TPU v7x, 32 devices: a whole 2x2x4 slice. The times are simulated.
32 devices in a mesh: dp: 8 (over z, x), mp: 4 (over y, core).
Axes of the slice: x: 2, y: 2, z: 4, core: 2. Of those that a mesh axis runs over, the one named last changes fastest.
Arguments:
- queries: bfloat16 [16, 16, 5120], P('dp', None, 'mp')
- key_value_cache: bfloat16 [128, 2, 128, 1024], P('dp', None, None, 'mp'), may hold values from -6 to 6
- slot_tags: int32 [128], P('dp'), may hold values from 0 to 15, as said below
- span_key_value: bfloat16 [16, 2, 16, 1024], P('dp', None, None, 'mp'), may hold values from -6 to 6
- answer_id: int32 [16], P('dp'), may hold values from 0 to 127
- w_cand: bfloat16 [5120, 128], P('mp')
Outputs:
- attended: bfloat16 [16, 16, 5120], P('dp', None, 'mp')
- chain_score: float32 [16], P('dp')
- answer_tally: float32 [1, 128], P(None, 'dp')
Inputs may be any that keep to these rules, and one draw needn't show every extreme that they name: `slot_tags`: among the 16 blocks of any one index of dp, at most 2 belong to the chains o * 2 to o * 2 + 1 of any one o, and for some o every index of dp holds exactly 2 such blocks. A chain may have no cached block.
All inputs are finite; a program needn't handle non-finite values.
Results may differ from a plain program's by a relative error of at most 0.0075.
Values may be sent and summed in bfloat16 or wider, within the bound.
No kernel may reach another device: no remote copies, remote signals or barrier semaphores. Data moves between devices by JAX's collectives and lax.ppermute only.
A program may use at most 128 MiB of HBM per device.

v0:
```python
import jax
import jax.numpy as jnp
from jax import lax
from jax.sharding import PartitionSpec as P

QUERY_HEADS = 40
KEY_VALUE_HEADS = 8
HEAD_SIZE = 128
NCAND = 128
PEER = 2
SAMPLES = 16
big_neg = -1e30


def block_terms(picked, blocks, causal):
    count = picked.shape[0]
    span = picked.shape[1]
    width = blocks.shape[2]
    heads_kv = blocks.shape[3] // HEAD_SIZE
    head_group = QUERY_HEADS // KEY_VALUE_HEADS
    query_rows = picked.reshape(count, span, heads_kv, head_group, HEAD_SIZE)
    lookup_matrix = blocks[:, 0].reshape(count, width, heads_kv, HEAD_SIZE)
    value_rows = blocks[:, 1].reshape(count, width, heads_kv, HEAD_SIZE)
    logit_rows = jnp.einsum(
        "nakgd,nbkd->nkgab", query_rows, lookup_matrix, preferred_element_type=jnp.float32
    ) * HEAD_SIZE ** (-0.5)
    if causal:
        allowed = jnp.arange(span)[:, None] >= jnp.arange(width)[None, :]
        logit_rows = jnp.where(allowed, logit_rows, big_neg)
    peaks = jnp.max(logit_rows, axis=-1)
    weights = jnp.exp(logit_rows - peaks[..., None])
    totals = jnp.sum(weights, axis=-1)
    summed_scores = jnp.einsum(
        "nkgab,nbkd->nkgad",
        weights.astype(jnp.bfloat16),
        value_rows,
        preferred_element_type=jnp.float32,
    )
    return (peaks, totals, summed_scores)


def merge_items(peaks, totals, summed_scores, member):
    member_f = member.astype(jnp.float32)
    masked = jnp.where(member[:, :, None, None, None], peaks[:, None], big_neg)
    chain_peak = jnp.max(masked, axis=0)
    item_peak = jnp.einsum("nc,ckga->nkga", member_f, chain_peak, precision=lax.Precision.HIGHEST)
    present = jnp.any(member, axis=1)
    factor = jnp.where(present[:, None, None, None], jnp.exp(peaks - item_peak), 0.0)
    chain_total = jnp.einsum(
        "nc,nkga->ckga", member_f, totals * factor, precision=lax.Precision.HIGHEST
    )
    chain_sum = jnp.einsum(
        "nc,nkgad->ckgad",
        member_f,
        summed_scores * factor[..., None],
        precision=lax.Precision.HIGHEST,
    )
    return (chain_peak, chain_total, chain_sum)


def fold_pair(first, second):
    overall = jnp.maximum(first[0], second[0])
    left = jnp.exp(first[0] - overall)
    right = jnp.exp(second[0] - overall)
    total = first[1] * left + second[1] * right
    summed_scores = first[2] * left[..., None] + second[2] * right[..., None]
    return (overall, total, summed_scores)


def per_device(queries, key_value_cache, slot_tags, span_key_value, answer_id, w_cand):
    accelerator_roster = lax.axis_size("dp")
    position = lax.axis_index("dp")
    chains_here = queries.shape[0]
    features = queries.shape[2]
    slots_here = slot_tags.shape[0]
    owner_index = slot_tags // chains_here
    chain_local = slot_tags % chains_here
    owner_hot = (
        owner_index[:, None] == jnp.arange(accelerator_roster, dtype=jnp.int32)[None, :]
    ).astype(jnp.int32)
    running = jnp.cumsum(owner_hot, axis=0) - 1
    rank_in = jnp.sum(owner_hot * running, axis=1)
    target = owner_index * PEER + rank_in
    places_all = accelerator_roster * PEER
    hit = (target[:, None] == jnp.arange(places_all, dtype=jnp.int32)[None, :]).astype(jnp.int32)
    source_row = jnp.sum(hit * jnp.arange(slots_here, dtype=jnp.int32)[:, None], axis=0)
    is_filled = jnp.sum(hit, axis=0) > 0
    send_chain = jnp.where(is_filled, jnp.sum(hit * chain_local[:, None], axis=0), chains_here)
    send_blocks = key_value_cache[source_row].reshape(
        (accelerator_roster, PEER) + key_value_cache.shape[1:]
    )
    send_chain = send_chain.reshape(accelerator_roster, PEER)
    blocks = lax.all_to_all(send_blocks, "dp", split_axis=0, concat_axis=0, tiled=True)
    places = lax.all_to_all(send_chain, "dp", split_axis=0, concat_axis=0, tiled=True)
    count = places.shape[0] * places.shape[1]
    flat_places = places.reshape(count)
    picked = queries[jnp.clip(flat_places, 0, chains_here - 1)]
    peaks, totals, summed_scores = block_terms(
        picked, blocks.reshape((count,) + blocks.shape[2:]), False
    )
    lead = places.shape
    peaks, totals, summed_scores, places = (
        peaks.reshape(lead + peaks.shape[1:]),
        totals.reshape(lead + totals.shape[1:]),
        summed_scores.reshape(lead + summed_scores.shape[1:]),
        places,
    )
    count = places.shape[0] * places.shape[1]
    member = places.reshape(count)[:, None] == jnp.arange(chains_here, dtype=jnp.int32)[None, :]
    remote = merge_items(
        peaks.reshape((count,) + peaks.shape[2:]),
        totals.reshape((count,) + totals.shape[2:]),
        summed_scores.reshape((count,) + summed_scores.shape[2:]),
        member,
    )
    own_span = block_terms(queries, span_key_value, True)
    final_peak, final_total, final_sum = fold_pair(own_span, remote)
    output = final_sum / final_total[..., None]
    output = jnp.transpose(output, (0, 3, 1, 2, 4)).reshape(chains_here, queries.shape[1], features)
    attended = output.astype(jnp.bfloat16)
    span = queries.shape[1]
    partial_logits = jnp.dot(
        attended.reshape(chains_here * span, features), w_cand, preferred_element_type=jnp.float32
    )
    logit_rows = lax.psum(partial_logits, "mp").reshape(chains_here, span, NCAND)
    top_logit = jnp.max(logit_rows, axis=-1, keepdims=True)
    log_norm = top_logit[..., 0] + jnp.log(jnp.sum(jnp.exp(logit_rows - top_logit), axis=-1))
    answer_hot = (answer_id[:, None] == jnp.arange(NCAND, dtype=jnp.int32)[None, :]).astype(
        jnp.float32
    )
    chosen_logit = jnp.sum(logit_rows * answer_hot[:, None, :], axis=-1)
    chain_score = jnp.mean(chosen_logit - log_norm, axis=-1)
    prompt_count = accelerator_roster * chains_here // SAMPLES
    global_chain = position * chains_here + jnp.arange(chains_here, dtype=jnp.int32)
    prompt_hot = (
        (global_chain // SAMPLES)[:, None] == jnp.arange(prompt_count, dtype=jnp.int32)[None, :]
    ).astype(jnp.float32)
    tally_terms = jnp.dot(
        prompt_hot.T, chain_score[:, None] * answer_hot, precision=lax.Precision.HIGHEST
    )
    answer_tally = lax.psum_scatter(tally_terms, "dp", scatter_dimension=1, tiled=True)
    return (attended, chain_score, answer_tally)


def solution(mesh):
    in_specs = (
        P("dp", None, "mp"),
        P("dp", None, None, "mp"),
        P("dp"),
        P("dp", None, None, "mp"),
        P("dp"),
        P("mp", None),
    )
    out_specs = (P("dp", None, "mp"), P("dp"), P(None, "dp"))
    return jax.shard_map(
        per_device, mesh=mesh, in_specs=in_specs, out_specs=out_specs, check_vma=False
    )
```

profile of v0, /device:TPU:0, one launch (start us, length us, event | category | flops | bytes accessed | tf_op | source)
XLA Modules:
  0.0 165.2 jit_solution(9929074711548436345)
XLA Ops:
  7.2 0.0 copy-start
  7.2 0.8 and_select_fusion.1
  8.0 0.1 fusion.28
  8.1 0.2 select_reduce_fusion.3
  8.3 0.1 convert_reduce_fusion
  8.4 0.7 select_n.71
  9.1 7.3 %all-to-all-start = ((s32[8,1,2]{2,1,0:T(1,128)}), s32[8,1,2]{2,1,0:T(1,128)S(1)}, u32[]{:S(2)}, u32[]{:S(2)}) async-start(s32[8,1,2]{2,1,0:T(1,128)} %bitcast.5), calls=%async_computation | async-start | bytes 8192 | tf_op jit(solution)/shard_map/all_to_all | solution.py:94
  16.4 0.0 copy-done
  16.4 2.0 %gather_fusion = bf16[16,2,128,256]{3,2,1,0:T(8,128)(2,1)} fusion(bf16[16,2,128,256]{3,2,1,0:T(8,128)(2,1)S(1)} %copy-done, s32[1024]{0:T(1024)S(1)} %pad_clamp_fusion.1), kind=kCustom, calls=%fused_computation | custom fusion | bytes 4194368 | tf_op jit(solution)/shard_map/gather | solution.py:89
  18.4 3.9 %copy.89 = bf16[8,2,2,128,256]{3,4,1,2,0:T(8,128)(2,1)} copy(bf16[8,2,2,128,256]{4,3,2,1,0:T(8,128)(2,1)} %bitcast.89) | data formatting | bytes 4194304 | tf_op jit(solution)/shard_map/reshape | solution.py:89
  22.3 0.0 copy-start.1
  22.3 0.0 copy-start.3
  22.3 0.0 copy-start.4
  22.3 0.5 all-to-all-done
  22.8 5.7 %all-to-all-start.1 = ((bf16[8,2,2,128,256]{3,4,1,2,0:T(8,128)(2,1)}), bf16[8,2,2,128,256]{3,4,1,2,0:T(8,128)(2,1)}, u32[]{:S(2)}, u32[]{:S(2)}) async-start(bf16[8,2,2,128,256]{3,4,1,2,0:T(8,128)(2,1)} %copy.89), calls=%async_computation.1 | async-start | bytes 4194304 | tf_op jit(solution)/shard_map/all_to_all | solution.py:93
  28.4 0.0 reduce-scatter.4.cloned.1.call-start
  28.5 0.0 copy-done.1
  28.5 0.1 reshape.174
  28.6 0.0 copy-done.3
  28.7 0.3 fusion.64
  29.0 0.1 fusion.18
  29.0 0.0 copy-done.4
  29.0 0.1 fusion.35
  29.1 0.5 broadcast.247
  29.6 0.7 fusion.60
  30.3 0.1 min.9
  30.4 1.4 gather_fusion.1
  31.8 1.8 %reshape.177 = bf16[16,16,2,5,128]{4,3,2,1,0:T(8,128)(2,1)S(1)} reshape(bf16[16,16,1280]{2,1,0:T(8,128)(2,1)} %gather_fusion.1) | data formatting | bytes 1310720 | tf_op jit(solution)/shard_map/reshape | solution.py:21
  33.6 0.1 eq.74
  33.7 42.5 %all-to-all-done.1 = bf16[8,2,2,128,256]{3,4,1,2,0:T(8,128)(2,1)} async-done(((bf16[8,2,2,128,256]{3,4,1,2,0:T(8,128)(2,1)}), bf16[8,2,2,128,256]{3,4,1,2,0:T(8,128)(2,1)}, u32[]{:S(2)}, u32[]{:S(2)}) %all-to-all-start.1) | async-done | bytes 2097184 | tf_op jit(solution)/shard_map/all_to_all | solution.py:93
  76.2 1.7 %copy.90 = bf16[8,2,2,128,256]{3,4,1,0,2:T(8,128)(2,1)S(1)} copy(bf16[8,2,2,128,256]{3,4,1,2,0:T(8,128)(2,1)} %all-to-all-done.1) | data formatting | bytes 4194304 | tf_op jit(solution)/shard_map/all_to_all | solution.py:93
  78.0 0.2 fusion.61
  78.2 0.6 fusion.63
  78.8 0.1 select_reduce_fusion
  78.9 0.2 fusion.12
  79.2 0.8 fusion.3
  80.0 1.4 convolution_multiply_fusion
  81.5 0.0 copy-start.2
  81.5 1.3 fusion.1
  82.8 0.2 fusion.14
  83.0 0.3 fusion.10
  83.3 0.1 convert_element_type.37
  83.4 0.0 copy-done.2
  83.4 0.2 fusion.65
  83.6 10.1 %psum.7 = f32[32,128]{1,0:T(8,128)S(1)} all-reduce(f32[32,128]{1,0:T(8,128)S(1)} %fusion.65), channel_id=1, replica_groups=mesh['dp'=8,'mp'=4] {'mp'}, use_global_device_ids=true, to_apply=%region_11.12 | all-reduce | flops 4096 | bytes 32768 | tf_op jit(solution)/shard_map/psum | solution.py:125
  93.7 0.1 reduce_max.45
  93.8 0.2 exponential_reduce_fusion
  94.0 0.1 sub.76
  94.1 0.1 reduce_sum.95
  94.2 0.0 copy-start.5
  94.3 1.0 convolution_bitcast_fusion.1
  95.2 0.0 reduce-scatter.4.cloned.1.call-update
  95.2 0.7 convert_element_type.36
  96.0 61.1 %reduce-scatter.4.cloned.1.call-done = f32[16,1]{1,0:T(8,128)} async-done(((f32[128,1]{1,0:T(8,128)}), f32[16,1]{1,0:T(8,128)}) %reduce-scatter.4.cloned.1.call-update) | async-done | bytes 80
  157.1 1.3 copy.124
  158.3 0.0 copy-done.5
  (21 shorter events, 0.3 us)
Async XLA Ops:
  7.2 9.2 %copy-start = (bf16[16,2,128,256]{3,2,1,0:T(8,128)(2,1)S(1)}, bf16[16,2,128,256]{3,2,1,0:T(8,128)(2,1)}, u32[]{:S(2)}) copy-start(bf16[16,2,128,256]{3,2,1,0:T(8,128)(2,1)} %param.7) | copy-start | bytes 6291460
  9.1 13.7 %all-to-all-start = ((s32[8,1,2]{2,1,0:T(1,128)}), s32[8,1,2]{2,1,0:T(1,128)S(1)}, u32[]{:S(2)}, u32[]{:S(2)}) async-start(s32[8,1,2]{2,1,0:T(1,128)} %bitcast.5), calls=%async_computation | async-start | bytes 8192 | tf_op jit(solution)/shard_map/all_to_all | solution.py:94
  22.3 6.2 %copy-start.1 = (bf16[2,16,1280]{2,1,0:T(8,128)(2,1)S(1)}, bf16[2,16,1280]{2,1,0:T(8,128)(2,1)}, u32[]{:S(2)}) copy-start(bf16[2,16,1280]{2,1,0:T(8,128)(2,1)} %param.6) | copy-start | bytes 245764
  22.3 6.3 %copy-start.3 = (bf16[2,2,16,256]{3,2,1,0:T(8,128)(2,1)S(1)}, bf16[2,2,16,256]{3,2,1,0:T(8,128)(2,1)}, u32[]{:S(2)}) copy-start(bf16[2,2,16,256]{3,2,1,0:T(8,128)(2,1)} %param.9) | copy-start | bytes 98308
  22.3 6.8 %copy-start.4 = (s32[2]{0:T(128)S(1)}, s32[2]{0:T(128)}, u32[]{:S(2)}) copy-start(s32[2]{0:T(128)} %param.10) | copy-start | bytes 28
  22.8 53.4 %all-to-all-start.1 = ((bf16[8,2,2,128,256]{3,4,1,2,0:T(8,128)(2,1)}), bf16[8,2,2,128,256]{3,4,1,2,0:T(8,128)(2,1)}, u32[]{:S(2)}, u32[]{:S(2)}) async-start(bf16[8,2,2,128,256]{3,4,1,2,0:T(8,128)(2,1)} %copy.89), calls=%async_computation.1 | async-start | bytes 4194304 | tf_op jit(solution)/shard_map/all_to_all | solution.py:93
  28.4 128.6 %reduce-scatter.4.cloned.1.call-start = ((), (), s32[]{:S(2)}) async-start(), calls=%async_computation.3 | async-start | bytes 73728
  81.5 1.9 %copy-start.2 = (bf16[1280,128]{1,0:T(8,128)(2,1)S(1)}, bf16[1280,128]{1,0:T(8,128)(2,1)}, u32[]{:S(2)}) copy-start(bf16[1280,128]{1,0:T(8,128)(2,1)} %param.11) | copy-start | bytes 983044
  94.2 64.1 %copy-start.5 = (f32[2]{0:T(128)}, f32[2]{0:T(128)S(1)}, u32[]{:S(2)}) copy-start(f32[2]{0:T(128)S(1)} %broadcast_multiply_fusion) | copy-start | bytes 28
Sparse Core Ops, SparseCore 0:
  95.4 61.6 reduce-scatter.3
where the time goes:
time: 166 us; the launch traced here: 165 us
  waiting for transfers between devices  104 us (63%)
  local copies, waits for them, and re-layouts  14.9 us (9%)
  between operations  14.3 us (9%)
  starting transfers between devices  13 us (8%)
  blocking collectives  10.1 us (6%)
  matrix products  5.37 us (3%)
  other arithmetic  3.42 us (2%)
    unnamed x2, waiting for transfers between devices  61.1 us
    all_to_all x1, waiting for transfers between devices, per_device(): lax.all_to_all(send_blocks, 'dp', split_axis=0, concat_axis=0, tiled=True)  42.5 us
    psum x1, blocking collectives, per_device(): lax.psum(partial_logits, 'mp').reshape(chains_here, span, NCAND)  10.1 us
    all_to_all x1, starting transfers between devices, per_device(): lax.all_to_all(send_chain, 'dp', split_axis=0, concat_axis=0, tiled=True)  7.28 us
    all_to_all x1, starting transfers between devices, per_device(): lax.all_to_all(send_blocks, 'dp', split_axis=0, concat_axis=0, tiled=True)  5.66 us
    reshape x1, local copies, waits for them, and re-layouts, per_device(): key_value_cache[source_row]  3.92 us
  transfers between devices with their start and end apart: 3, of which 3 were waited for; matrix products, arithmetic and copies ran while one was open for 7% of the time, Pallas kernels for 0%

commit v1 on v0

--- a/solution.py
+++ b/solution.py
@@ -10,6 +10,29 @@
 PEER = 2
 SAMPLES = 16
 big_neg = -1e30
+
+
+def split_up(value, dim, count):
+    lengths = value.shape
+    blocks = value.reshape(*lengths[:dim], count, lengths[dim] // count, *lengths[dim + 1 :])
+    return jnp.moveaxis(blocks, dim, 0)
+
+
+def in_order(parts, dim):
+    parts = jnp.moveaxis(parts, 0, dim)
+    shape = parts.shape
+    return parts.reshape(*shape[:dim], shape[dim] * shape[dim + 1], *shape[dim + 2 :])
+
+
+def swapped_with_each(x, axis, split_dim, concat_dim):
+    size, index = (lax.axis_size(axis), lax.axis_index(axis))
+    blocks = split_up(x, split_dim, size)
+    gathered = [blocks[index]]
+    for step in range(1, size):
+        sent = blocks[index ^ step]
+        gathered.append(lax.ppermute(sent, axis, [(i, i ^ step) for i in range(size)]))
+    blocks = jnp.stack(gathered)[index ^ jnp.arange(size)]
+    return in_order(blocks, concat_dim)
 
 
 def block_terms(picked, blocks, causal):
@@ -90,7 +113,7 @@
         (accelerator_roster, PEER) + key_value_cache.shape[1:]
     )
     send_chain = send_chain.reshape(accelerator_roster, PEER)
-    blocks = lax.all_to_all(send_blocks, "dp", split_axis=0, concat_axis=0, tiled=True)
+    blocks = swapped_with_each(send_blocks, "dp", 0, 0)
     places = lax.all_to_all(send_chain, "dp", split_axis=0, concat_axis=0, tiled=True)
     count = places.shape[0] * places.shape[1]
     flat_places = places.reshape(count)

time: 166 us -> 183 us (1.10)
  local copies, waits for them, and re-layouts: 14.9 us -> 35.9 us
  waiting for transfers between devices: 104 us -> 88.7 us
  starting transfers between devices: 13 us -> 19.1 us
  other arithmetic: 3.42 us -> 6.28 us
  matrix products: 5.37 us -> 7.76 us
    all_to_all x1 -> x0, waiting for transfers between devices: 42.5 us -> none  [per_device(): lax.all_to_all(send_blocks, 'dp', split_axis=0, concat_axis=0, tiled=True)]
    ppermute x0 -> x7, waiting for transfers between devices: none -> 20.3 us  [swapped_with_each(): lax.ppermute(sent, axis, [(i, i ^ step) for i in range(size)])]
    unnamed x13 -> x45, local copies, waits for them, and re-layouts: 1.31 us -> 14.7 us
    ppermute x0 -> x7, starting transfers between devices: none -> 11.8 us  [swapped_with_each(): lax.ppermute(sent, axis, [(i, i ^ step) for i in range(size)])]
    unnamed x2, waiting for transfers between devices: 61.1 us -> 67.3 us
    all_to_all x1 -> x0, starting transfers between devices: 5.66 us -> none  [per_device(): lax.all_to_all(send_blocks, 'dp', split_axis=0, concat_axis=0, tiled=True)]
    reshape x1 -> x0, local copies, waits for them, and re-layouts: 3.92 us -> none  [per_device(): key_value_cache[source_row]]
    gather x0 -> x1, local copies, waits for them, and re-layouts: none -> 3.56 us  [swapped_with_each(): blocks = jnp.stack(gathered)[index ^ jnp.arange(size)]]
  transfers between devices with their start and end apart: 3 -> 9, of which waited for: 3 -> 4; matrix products, arithmetic and copies ran while one was open for 7% -> 10% of each run, Pallas kernels for 0% -> 0%
where the time goes in v1:
time: 183 us; the launch traced here: 182 us
  waiting for transfers between devices  88.7 us (48%)
  local copies, waits for them, and re-layouts  35.9 us (20%)
  starting transfers between devices  19.1 us (10%)
  between operations  14.4 us (8%)
  blocking collectives  10.1 us (6%)
  matrix products  7.76 us (4%)
  other arithmetic  6.28 us (3%)
    unnamed x2, waiting for transfers between devices  67.3 us
    ppermute x7, waiting for transfers between devices, swapped_with_each(): lax.ppermute(sent, axis, [(i, i ^ step) for i in range(size)])  20.3 us
    unnamed x45, local copies, waits for them, and re-layouts  14.7 us
    ppermute x7, starting transfers between devices, swapped_with_each(): lax.ppermute(sent, axis, [(i, i ^ step) for i in range(size)])  11.8 us
    psum x1, blocking collectives, per_device(): lax.psum(partial_logits, 'mp').reshape(chains_here, span, NCAND)  10.1 us
    all_to_all x1, starting transfers between devices, per_device(): lax.all_to_all(send_chain, 'dp', split_axis=0, concat_axis=0, tiled=True)  7.28 us
  transfers between devices with their start and end apart: 9, of which 4 were waited for; matrix products, arithmetic and copies ran while one was open for 10% of the time, Pallas kernels for 0%

profile of v1, /device:TPU:0, one launch (start us, length us, event | category | flops | bytes accessed | tf_op | source)
XLA Modules:
  0.0 182.3 jit_solution(14513685660029986573)
XLA Ops:
  7.2 0.8 and_select_fusion.1
  8.1 0.2 select_reduce_fusion.3
  8.3 0.1 convert_reduce_fusion
  8.4 0.7 select_n.105
  9.1 7.3 %all-to-all-start = ((s32[8,1,2]{2,1,0:T(1,128)}), s32[8,1,2]{2,1,0:T(1,128)S(1)}, u32[]{:S(2)}, u32[]{:S(2)}) async-start(s32[8,1,2]{2,1,0:T(1,128)} %bitcast.5), calls=%async_computation | async-start | bytes 8192 | tf_op jit(solution)/shard_map/all_to_all | solution.py:117
  16.5 0.7 fusion.62
  17.2 1.0 reshape.184
  18.2 0.6 reshape_squeeze.13
  18.9 1.3 fusion.35
  20.2 0.3 fusion.64
  20.5 0.7 copy-done.2
  21.1 0.7 fusion.18
  21.8 1.1 all-to-all-done
  22.9 0.5 broadcast.282
  23.4 0.7 fusion.60
  24.0 0.1 min.9
  24.1 2.0 %gather_fusion = bf16[16,2,128,256]{3,2,1,0:T(8,128)(2,1)} fusion(bf16[16,2,128,256]{3,2,1,0:T(8,128)(2,1)S(1)} %copy-done, s32[1024]{0:T(1024)S(1)} %pad_clamp_fusion.2), kind=kCustom, calls=%fused_computation | custom fusion | bytes 4194368 | tf_op jit(solution)/shard_map/gather | solution.py:112
  26.1 2.7 %dynamic-slice_bitcast_fusion = (bf16[1,2,2,128,256]{4,3,2,1,0:T(8,128)(2,1)S(1)}, bf16[1,2,2,128,256]{4,3,2,1,0:T(8,128)(2,1)S(1)}, bf16[1,2,2,128,256]{4,3,2,1...) fusion(bf16[8,1,2,2,128,256]{5,4,3,2,0,1:T(8,128)(2,1)} %bitcas, ...), kind=kLoop, calls=%fused_computation.35 | loop fusion | bytes 4194336 | tf_op jit(solution)/shard_map/squeeze | solution.py:32
  28.8 0.9 collective-permute-start
  29.7 1.5 collective-permute-start.1
  31.2 1.1 collective-permute-start.2
  32.3 1.8 collective-permute-start.3
  34.1 1.5 collective-permute-start.4
  35.6 1.0 iota_compare_fusion.5
  36.7 0.6 gather_fusion.2
  37.3 1.7 reshape.185
  39.0 3.3 %collective-permute-start.5 = (bf16[1,2,2,128,256]{4,3,2,1,0:T(8,128)(2,1)S(1)}, bf16[1,2,2,128,256]{4,3,2,1,0:T(8,128)(2,1)S(1)}, u32[]{:S(2)}, u32[]{:S(2)}) collective-permute-start(bf16[1,2,2,128,256]{4,3,2,1,0:T(8,128)(2,1)S(1)} %get-tuple-element.13), channel_id=1, source_target_pairs={{0,24},{4,28},{8,16},{12,20},{16,8},{20,12},{24,0},{28,4},{1,25},{... | collective-permute-start | bytes 786440 | tf_op jit(solution)/shard_map/ppermute | solution.py:33
  42.3 1.7 bitcast_dynamic-update-slice_fusion.6
  43.9 4.7 %collective-permute-done.1 = bf16[1,2,2,128,256]{4,3,2,1,0:T(8,128)(2,1)} collective-permute-done((bf16[1,2,2,128,256]{4,3,2,1,0:T(8,128)(2,1)}, bf16[1,2,2,128,256]{4,3,2,1,0:T(8,128)(2,1)}, u32[]{:S(2)}, u32[]{:S(2)}) %collective-permute-start.1) | collective-permute-done | bytes 262176 | tf_op jit(solution)/shard_map/ppermute | solution.py:33
  48.7 1.8 %collective-permute-start.6 = (bf16[1,2,2,128,256]{4,3,2,1,0:T(8,128)(2,1)S(1)}, bf16[1,2,2,128,256]{4,3,2,1,0:T(8,128)(2,1)S(1)}, u32[]{:S(2)}, u32[]{:S(2)}) collective-permute-start(bf16[1,2,2,128,256]{4,3,2,1,0:T(8,128)(2,1)S(1)} %get-tuple-element.12), channel_id=1, source_target_pairs={{0,28},{4,24},{8,20},{12,16},{16,12},{20,8},{24,4},{28,0},{1,29},{... | collective-permute-start | bytes 786440 | tf_op jit(solution)/shard_map/ppermute | solution.py:33
  50.5 1.7 bitcast_dynamic-update-slice_fusion.5
  52.2 1.7 bitcast_dynamic-update-slice_fusion.4
  53.9 1.7 bitcast_dynamic-update-slice_fusion.3
  55.5 15.6 %collective-permute-done.4 = bf16[1,2,2,128,256]{4,3,2,1,0:T(8,128)(2,1)} collective-permute-done((bf16[1,2,2,128,256]{4,3,2,1,0:T(8,128)(2,1)}, bf16[1,2,2,128,256]{4,3,2,1,0:T(8,128)(2,1)}, u32[]{:S(2)}, u32[]{:S(2)}) %collective-permute-start.4) | collective-permute-done | bytes 262176 | tf_op jit(solution)/shard_map/ppermute | solution.py:33
  71.1 1.7 bitcast_dynamic-update-slice_fusion.2
  72.8 0.7 bitcast_dynamic-update-slice_fusion.1
  73.5 0.7 bitcast_dynamic-update-slice_fusion
  74.3 3.6 %gather_fusion.1 = bf16[8,2,2,128,256]{4,3,2,1,0:T(8,128)(2,1)} fusion(bf16[8,2,2,128,256]{4,3,2,1,0:T(8,128)(2,1)} %bitcast.122, s32[1024]{0:T(1024)S(1)} %pad_clamp_fusion.1), kind=kCustom, calls=%fused_computation.1 | custom fusion | bytes 4194336 | tf_op jit(solution)/shard_map/gather | solution.py:34
  77.8 2.7 %fusion.61 = (bf16[16,1,128,256]{3,2,1,0:T(8,128)(2,1)S(1)}, bf16[16,1,128,256]{3,2,1,0:T(8,128)(2,1)}) fusion(bf16[16,2,128,256]{3,2,1,0:T(8,128)(2,1)} %bitcast.120), kind=kLoop, calls=%fused_computation.123 | loop fusion | bytes 4194304 | tf_op jit(solution)/shard_map/slice | solution.py:45
  80.5 1.3 copy.143
  81.9 2.1 %fusion.63 = (f32[16,2,5,16]{3,2,1,0:T(8,128)S(1)}, f32[16,2,5,16,128]{4,3,2,1,0:T(8,128)S(1)}) fusion(bf16[16,128,2,128,1]{1,3,4,2,0:T(8,128)(2,1)} %bitcast.121, bf16[16,16,2,5,128]{4,3,2,1,0:T(8,128)(2,1)} %reshape.185), kind=kOutput, calls=%fused_computation.125 | convolution fusion | flops 84538880 | bytes 3024896 | tf_op jit(solution)/shard_map/nakgd,nbkd->nkgab/dot_general | solution.py:47
  84.1 0.8 fusion.3
  84.9 0.1 select_reduce_fusion
  85.0 0.2 fusion.12
  85.3 0.7 copy.117
  86.0 0.6 copy.112
  86.6 0.6 copy.120
  87.2 0.2 fusion.14
  87.3 0.6 copy.123
  87.9 2.3 %copy.144 = bf16[16,1,128,256]{2,3,0,1:T(8,128)(2,1)} copy(bf16[16,1,128,256]{3,2,1,0:T(8,128)(2,1)} %get-tuple-element.11) | data formatting | bytes 2097152
  90.3 2.3 %convolution_multiply_fusion = f32[16,2,5,16,128]{4,3,2,1,0:T(8,128)S(1)} fusion(bf16[16,128,2,128,1]{1,3,4,2,0:T(8,128)(2,1)} %bitcast.123, f32[16,2,5,16,128]{4,3,2,1,0:T(8,128)S(1)} %get-tuple-element.29, f32[16,2,5,16]{3,2,1,0:T(8,128)} %copy.117, f32[16,2,5,16]{3,2,1,0:T(8,128)S(1)} %get-tuple-element.28), kind=kOutput, calls=%fused_computation.3 | convolution fusion | flops 84869120 | bytes 3690496 | tf_op jit(solution)/shard_map/nkgab,nbkd->nkgad/dot_general | solution.py:56
  92.6 1.3 fusion.1
  93.9 0.3 fusion.10
  94.2 0.1 convert_element_type.37
  94.3 0.2 fusion.66
  94.5 10.1 %psum.7 = f32[32,128]{1,0:T(8,128)S(1)} all-reduce(f32[32,128]{1,0:T(8,128)S(1)} %fusion.66), channel_id=1, replica_groups=mesh['dp'=8,'mp'=4] {'mp'}, use_global_device_ids=true, to_apply=%region_11.12 | all-reduce | flops 4096 | bytes 32768 | tf_op jit(solution)/shard_map/psum | solution.py:148
  104.6 0.1 reduce_max.45
  104.8 0.2 exponential_reduce_fusion
  105.0 0.1 sub.76
  105.0 0.1 reduce_sum.95
  105.2 1.0 convolution_bitcast_fusion.1
  106.2 0.7 convert_element_type.36
  106.9 67.3 %reduce-scatter.4.cloned.1.call-done = f32[16,1]{1,0:T(8,128)} async-done(((f32[128,1]{1,0:T(8,128)}), f32[16,1]{1,0:T(8,128)}) %reduce-scatter.4.cloned.1.call-update) | async-done | bytes 80
  174.2 1.3 copy.142
  (59 shorter events, 0.5 us)
Async XLA Ops:
  7.2 17.0 %copy-start = (bf16[16,2,128,256]{3,2,1,0:T(8,128)(2,1)S(1)}, bf16[16,2,128,256]{3,2,1,0:T(8,128)(2,1)}, u32[]{:S(2)}) copy-start(bf16[16,2,128,256]{3,2,1,0:T(8,128)(2,1)} %param.7) | copy-start | bytes 6291460
  9.1 13.8 %all-to-all-start = ((s32[8,1,2]{2,1,0:T(1,128)}), s32[8,1,2]{2,1,0:T(1,128)S(1)}, u32[]{:S(2)}, u32[]{:S(2)}) async-start(s32[8,1,2]{2,1,0:T(1,128)} %bitcast.5), calls=%async_computation | async-start | bytes 8192 | tf_op jit(solution)/shard_map/all_to_all | solution.py:117
  16.4 157.9 %reduce-scatter.4.cloned.1.call-start = ((), (), s32[]{:S(2)}) async-start(), calls=%async_computation.2 | async-start | bytes 73728
  20.5 0.7 copy-start.2
  26.1 10.6 %copy-start.1 = (bf16[2,16,1280]{2,1,0:T(8,128)(2,1)S(1)}, bf16[2,16,1280]{2,1,0:T(8,128)(2,1)}, u32[]{:S(2)}) copy-start(bf16[2,16,1280]{2,1,0:T(8,128)(2,1)} %param.6) | copy-start | bytes 245764
  28.8 10.2 %collective-permute-start = (bf16[1,2,2,128,256]{4,3,2,1,0:T(8,128)(2,1)}, bf16[1,2,2,128,256]{4,3,2,1,0:T(8,128)(2,1)}, u32[]{:S(2)}, u32[]{:S(2)}) collective-permute-start(bf16[1,2,2,128,256]{4,3,2,1,0:T(8,128)(2,1)} %get-tuple-element.18), channel_id=1, source_target_pairs={{0,4},{4,0},{8,12},{12,8},{16,20},{20,16},{24,28},{28,24},{1,5},{5... | collective-permute-start | bytes 786440 | tf_op jit(solution)/shard_map/ppermute | solution.py:33
  29.7 18.9 %collective-permute-start.1 = (bf16[1,2,2,128,256]{4,3,2,1,0:T(8,128)(2,1)}, bf16[1,2,2,128,256]{4,3,2,1,0:T(8,128)(2,1)}, u32[]{:S(2)}, u32[]{:S(2)}) collective-permute-start(bf16[1,2,2,128,256]{4,3,2,1,0:T(8,128)(2,1)} %get-tuple-element.17), channel_id=1, source_target_pairs={{0,8},{4,12},{8,0},{12,4},{16,24},{20,28},{24,16},{28,20},{1,9},{5... | collective-permute-start | bytes 786440 | tf_op jit(solution)/shard_map/ppermute | solution.py:33
  31.2 21.0 %collective-permute-start.2 = (bf16[1,2,2,128,256]{4,3,2,1,0:T(8,128)(2,1)}, bf16[1,2,2,128,256]{4,3,2,1,0:T(8,128)(2,1)}, u32[]{:S(2)}, u32[]{:S(2)}) collective-permute-start(bf16[1,2,2,128,256]{4,3,2,1,0:T(8,128)(2,1)} %get-tuple-element.16), channel_id=1, source_target_pairs={{0,12},{4,8},{8,4},{12,0},{16,28},{20,24},{24,20},{28,16},{1,13},{... | collective-permute-start | bytes 786440 | tf_op jit(solution)/shard_map/ppermute | solution.py:33
  32.3 21.5 %collective-permute-start.3 = (bf16[1,2,2,128,256]{4,3,2,1,0:T(8,128)(2,1)}, bf16[1,2,2,128,256]{4,3,2,1,0:T(8,128)(2,1)}, u32[]{:S(2)}, u32[]{:S(2)}) collective-permute-start(bf16[1,2,2,128,256]{4,3,2,1,0:T(8,128)(2,1)} %get-tuple-element.15), channel_id=1, source_target_pairs={{0,16},{4,20},{8,24},{12,28},{16,0},{20,4},{24,8},{28,12},{1,17},{... | collective-permute-start | bytes 786440 | tf_op jit(solution)/shard_map/ppermute | solution.py:33
  34.1 37.0 %collective-permute-start.4 = (bf16[1,2,2,128,256]{4,3,2,1,0:T(8,128)(2,1)}, bf16[1,2,2,128,256]{4,3,2,1,0:T(8,128)(2,1)}, u32[]{:S(2)}, u32[]{:S(2)}) collective-permute-start(bf16[1,2,2,128,256]{4,3,2,1,0:T(8,128)(2,1)} %get-tuple-element.14), channel_id=1, source_target_pairs={{0,20},{4,16},{8,28},{12,24},{16,4},{20,0},{24,12},{28,8},{1,21},{... | collective-permute-start | bytes 786440 | tf_op jit(solution)/shard_map/ppermute | solution.py:33
  35.6 18.2 %copy-start.10 = (s32[16]{0:T(128)}, s32[16]{0:T(128)S(1)}, u32[]{:S(2)}) copy-start(s32[16]{0:T(128)S(1)} %eq.74) | copy-start | bytes 196
  39.0 33.8 %collective-permute-start.5 = (bf16[1,2,2,128,256]{4,3,2,1,0:T(8,128)(2,1)S(1)}, bf16[1,2,2,128,256]{4,3,2,1,0:T(8,128)(2,1)S(1)}, u32[]{:S(2)}, u32[]{:S(2)}) collective-permute-start(bf16[1,2,2,128,256]{4,3,2,1,0:T(8,128)(2,1)S(1)} %get-tuple-element.13), channel_id=1, source_target_pairs={{0,24},{4,28},{8,16},{12,20},{16,8},{20,12},{24,0},{28,4},{1,25},{... | collective-permute-start | bytes 786440 | tf_op jit(solution)/shard_map/ppermute | solution.py:33
  48.7 24.9 %collective-permute-start.6 = (bf16[1,2,2,128,256]{4,3,2,1,0:T(8,128)(2,1)S(1)}, bf16[1,2,2,128,256]{4,3,2,1,0:T(8,128)(2,1)S(1)}, u32[]{:S(2)}, u32[]{:S(2)}) collective-permute-start(bf16[1,2,2,128,256]{4,3,2,1,0:T(8,128)(2,1)S(1)} %get-tuple-element.12), channel_id=1, source_target_pairs={{0,28},{4,24},{8,20},{12,16},{16,12},{20,8},{24,4},{28,0},{1,29},{... | collective-permute-start | bytes 786440 | tf_op jit(solution)/shard_map/ppermute | solution.py:33
  81.9 3.0 %copy-start.15 = (pred[16,2]{0,1:T(4,128)(4,1)S(1)}, pred[16,2]{0,1:T(4,128)(4,1)}, u32[]{:S(2)}) copy-start(pred[16,2]{0,1:T(4,128)(4,1)} %get-tuple-element.24) | copy-start | bytes 100
  81.9 3.1 %copy-start.11 = (s32[16]{0:T(128)S(1)}, s32[16]{0:T(128)}, u32[]{:S(2)}) copy-start(s32[16]{0:T(128)} %copy-done.10) | copy-start | bytes 196
  81.9 3.2 %copy-start.14 = (pred[16]{0:T(512)(128)(4,1)S(1)}, pred[16]{0:T(512)(128)(4,1)}, u32[]{:S(2)}) copy-start(pred[16]{0:T(512)(128)(4,1)} %get-tuple-element.25) | copy-start | bytes 52
  81.9 5.3 %copy-start.5 = (f32[2,2,5,16]{3,2,1,0:T(8,128)S(1)}, f32[2,2,5,16]{3,2,1,0:T(8,128)}, u32[]{:S(2)}) copy-start(f32[2,2,5,16]{3,2,1,0:T(8,128)} %fusion.18) | copy-start | bytes 3844
  90.2 2.3 %copy-start.12 = (s32[16]{0:T(128)S(1)}, s32[16]{0:T(128)}, u32[]{:S(2)}) copy-start(s32[16]{0:T(128)} %copy-done.10) | copy-start | bytes 196
  90.2 3.6 %copy-start.3 = (f32[2,2,5,16,16]{3,4,2,1,0:T(8,128)S(1)}, f32[2,2,5,16,16]{3,4,2,1,0:T(8,128)}, u32[]{:S(2)}) copy-start(f32[2,2,5,16,16]{3,4,2,1,0:T(8,128)} %copy-done.2) | copy-start | bytes 61444
  90.2 3.6 %copy-start.6 = (bf16[2,16,2,128]{3,2,1,0:T(2,128)(2,1)S(1)}, bf16[2,16,2,128]{3,2,1,0:T(2,128)(2,1)}, u32[]{:S(2)}) copy-start(bf16[2,16,2,128]{3,2,1,0:T(2,128)(2,1)} %reshape_squeeze.13) | copy-start | bytes 49156
  90.2 3.6 %copy-start.7 = (f32[2,16,2,5]{1,3,2,0:T(8,128)S(1)}, f32[2,16,2,5]{1,3,2,0:T(8,128)}, u32[]{:S(2)}) copy-start(f32[2,16,2,5]{1,3,2,0:T(8,128)} %copy.112) | copy-start | bytes 3844
  90.2 3.6 %copy-start.8 = (f32[2,16,2,5]{1,3,2,0:T(8,128)S(1)}, f32[2,16,2,5]{1,3,2,0:T(8,128)}, u32[]{:S(2)}) copy-start(f32[2,16,2,5]{1,3,2,0:T(8,128)} %copy.120) | copy-start | bytes 3844
  90.3 3.6 %copy-start.9 = (f32[2,16,2,5]{1,3,2,0:T(8,128)S(1)}, f32[2,16,2,5]{1,3,2,0:T(8,128)}, u32[]{:S(2)}) copy-start(f32[2,16,2,5]{1,3,2,0:T(8,128)} %copy.123) | copy-start | bytes 3844
  92.5 1.8 copy-start.4
  92.6 12.2 %copy-start.13 = (f32[2,128]{1,0:T(2,128)S(1)}, f32[2,128]{1,0:T(2,128)}, u32[]{:S(2)}) copy-start(f32[2,128]{1,0:T(2,128)} %fusion.35) | copy-start | bytes 3076
  92.6 12.6 %copy-start.16 = (s32[2]{0:T(128)S(1)}, s32[2]{0:T(128)}, u32[]{:S(2)}) copy-start(s32[2]{0:T(128)} %param.10) | copy-start | bytes 28
  105.2 70.3 %copy-start.17 = (f32[2]{0:T(128)}, f32[2]{0:T(128)S(1)}, u32[]{:S(2)}) copy-start(f32[2]{0:T(128)S(1)} %broadcast_multiply_fusion) | copy-start | bytes 28
Sparse Core Ops, SparseCore 0:
  106.3 67.8 reduce-scatter.3
